TPU v7x, 8 devices: a whole 2x2x1 slice. The times are simulated.
8 devices in a mesh: dp: 1 (over z), tp: 2 (over y), cp: 4 (over x, core).
Axes of the slice: x: 2, y: 2, z: 1, core: 2. Of those that a mesh axis runs over, the one named last changes fastest.
Arguments:
- hidden: bfloat16 [16, 512, 6144], P('dp', 'cp')
- alphas: float32 [2], replicated
- wq_attn: bfloat16 [6144, 8192], P(None, 'tp')
- wk_attn: bfloat16 [6144, 1024], P(None, 'tp')
- wv_attn: bfloat16 [6144, 1024], P(None, 'tp')
- wo_attn: bfloat16 [8192, 6144], P('tp')
- gain_attn: float32 [6144], replicated
- wq_lin: bfloat16 [6144, 8192], P(None, 'tp')
- wk_lin: bfloat16 [6144, 8192], P(None, 'tp')
- wv_lin: bfloat16 [6144, 8192], P(None, 'tp')
- wg_lin: bfloat16 [6144, 8192], P(None, 'tp')
- slopes: float32 [64], P('tp')
- gain_inner: float32 [8192], P('tp')
- wo_lin: bfloat16 [8192, 6144], P('tp')
- gain_lin: float32 [6144], replicated
Outputs:
- output: bfloat16 [16, 512, 6144], P('dp', 'cp')
All inputs are finite; a program needn't handle non-finite values.
Results may differ from a plain program's by a relative error of at most 0.0125434.
Values are sent between devices in bfloat16 or wider.
A program may use at most 1.75 GiB of HBM per device.

v0:
```python
import math
import jax
import jax.numpy as jnp
from jax import lax
from jax.sharding import PartitionSpec as P

ROPE_BASE = 10000000.0
NORM_EPS = 1e-5


def rms_norm(values, gain_vec):
    return values * lax.rsqrt(jnp.mean(values * values, axis=-1, keepdims=True) + NORM_EPS) * gain_vec


def rotary(values, positions):
    rot_dims = values.shape[-1] // 2
    half = rot_dims // 2
    inv_freq = jnp.power(ROPE_BASE, -jnp.arange(half, dtype=jnp.float32) * 2.0 / rot_dims)
    angles = positions.astype(jnp.float32)[:, None] * inv_freq[None, :]
    cosine = jnp.cos(angles)[:, None, :]
    sine = jnp.sin(angles)[:, None, :]
    first = values[..., :half]
    second = values[..., half:rot_dims]
    return jnp.concatenate([first * cosine - second * sine, second * cosine + first * sine, values[..., rot_dims:]], axis=-1)


def attention_inputs(hidden, wq_attn, wk_attn, wv_attn, positions, head_dim):
    n_batch = hidden.shape[0]
    n_tok = hidden.shape[1]
    kv_heads = wk_attn.shape[1] // head_dim
    group = wq_attn.shape[1] // wk_attn.shape[1]
    q_proj = jnp.einsum('btm,mn->btn', hidden, wq_attn, preferred_element_type=jnp.float32)
    queries = rotary(q_proj.reshape(n_batch, n_tok, kv_heads * group, head_dim), positions).astype(jnp.bfloat16)
    k_proj = jnp.einsum('btm,mn->btn', hidden, wk_attn, preferred_element_type=jnp.float32)
    keys = rotary(k_proj.reshape(n_batch, n_tok, kv_heads, head_dim), positions).astype(jnp.bfloat16)
    values = jnp.einsum('btm,mn->btn', hidden, wv_attn, preferred_element_type=jnp.float32).astype(jnp.bfloat16)
    return queries.reshape(n_batch, n_tok, kv_heads, group, head_dim), keys, values.reshape(n_batch, n_tok, kv_heads, head_dim)


def softmax_init(queries):
    stats_shape = (queries.shape[0], queries.shape[2], queries.shape[3], queries.shape[1])
    return (jnp.full(stats_shape, -jnp.inf, jnp.float32), jnp.zeros(stats_shape, jnp.float32), jnp.zeros(stats_shape + (queries.shape[4],), jnp.float32))


def softmax_update(carry, queries, key_blk, value_blk, mask, scale):
    run_max, run_total, out_acc = carry
    scores = jnp.einsum('bqkgd,bskd->bkgqs', queries, key_blk, preferred_element_type=jnp.float32) * scale
    if mask is not None:
        scores = jnp.where(mask, scores, -jnp.inf)
    new_max = jnp.maximum(run_max, jnp.max(scores, axis=-1))
    factor = jnp.exp(run_max - new_max)
    prob_vals = jnp.exp(scores - new_max[..., None])
    run_total = run_total * factor + jnp.sum(prob_vals, axis=-1)
    out_acc = out_acc * factor[..., None] + jnp.einsum('bkgqs,bskd->bkgqd', prob_vals.astype(jnp.bfloat16), value_blk, preferred_element_type=jnp.float32)
    return new_max, run_total, out_acc


def attention_partial(carry, wo_attn):
    attn_vals = (carry[2] / carry[1][..., None]).astype(jnp.bfloat16)
    w_out = wo_attn.reshape(attn_vals.shape[1], attn_vals.shape[2], attn_vals.shape[4], wo_attn.shape[1])
    return jnp.einsum('bkgqd,kgdm->bqm', attn_vals, w_out, preferred_element_type=jnp.float32)


def lightning_inputs(mid_hidden, wq_lin, wk_lin, wv_lin, wg_lin, n_heads):
    n_batch = mid_hidden.shape[0]
    n_tok = mid_hidden.shape[1]

    def heads_of(weight):
        projected = jnp.einsum('btm,mn->btn', mid_hidden, weight, preferred_element_type=jnp.float32)
        return jax.nn.silu(projected).astype(jnp.bfloat16).reshape(n_batch, n_tok, n_heads, weight.shape[1] // n_heads)

    gate_vals = jax.nn.sigmoid(jnp.einsum('btm,mn->btn', mid_hidden, wg_lin, preferred_element_type=jnp.float32))
    return heads_of(wq_lin), heads_of(wk_lin), heads_of(wv_lin), gate_vals


def lightning_local(queries, keys, values, rates, tile):
    n_batch, n_tok, n_heads, head_dim = queries.shape
    n_tiles = n_tok // tile
    tiled_shape = (n_batch, n_tiles, tile, n_heads, head_dim)
    q_tiles = queries.reshape(tiled_shape)
    k_tiles = keys.reshape(tiled_shape)
    v_tiles = values.reshape(tiled_shape).astype(jnp.float32)
    offsets = jnp.arange(tile, dtype=jnp.float32)
    tok_gap = offsets[:, None] - offsets[None, :]
    intra_w = jnp.where(tok_gap >= 0, jnp.exp(-rates[:, None, None] * jnp.maximum(tok_gap, 0.0)), 0.0)
    scores = jnp.einsum('bnqhd,bnshd->bnhqs', q_tiles, k_tiles, preferred_element_type=jnp.float32) * intra_w
    inside = jnp.einsum('bnhqs,bnshd->bnqhd', scores, v_tiles)
    key_decay = jnp.exp(-rates[None, :] * (tile - 1.0 - offsets[:, None]))
    tile_states = jnp.einsum('bnshd,bnshe->bnhde', k_tiles * key_decay[:, :, None], v_tiles)
    tile_idx = jnp.arange(n_tiles, dtype=jnp.float32)
    tile_gap = tile_idx[:, None] - 1.0 - tile_idx[None, :]
    chain_w = jnp.where(tile_gap >= 0, jnp.exp(-rates[:, None, None] * tile * jnp.maximum(tile_gap, 0.0)), 0.0)
    entering = jnp.einsum('hnm,bmhde->bnhde', chain_w, tile_states)
    query_decay = jnp.exp(-rates[None, :] * (offsets[:, None] + 1.0))
    carried = jnp.einsum('bnqhd,bnhde->bnqhe', q_tiles.astype(jnp.float32), entering) * query_decay[:, :, None]
    end_w = jnp.exp(-rates[:, None] * tile * (n_tiles - 1.0 - tile_idx[None, :]))
    end_state = jnp.einsum('hn,bnhde->bhde', end_w, tile_states)
    return (inside + carried).reshape(queries.shape), end_state


def from_earlier(queries, prior_state, rates):
    steps = jnp.arange(queries.shape[1], dtype=jnp.float32) + 1.0
    weight = jnp.exp(-rates[None, :] * steps[:, None])
    return jnp.einsum('bthd,bhde->bthe', queries.astype(jnp.float32), prior_state) * weight[:, :, None]


def solution(mesh):
    cp_size = mesh.shape['cp']
    tp_size = mesh.shape['tp']
    shift = [(src, src + 1) for src in range(cp_size - 1)]
    tile = 128

    def body(hidden, alphas, wq_attn, wk_attn, wv_attn, wo_attn, gain_attn, wq_lin, wk_lin, wv_lin, wg_lin, slopes, gain_inner, wo_lin, gain_lin):
        n_heads = slopes.shape[0]
        head_dim = wq_lin.shape[1] // n_heads
        n_tok = hidden.shape[1]
        cp_idx = lax.axis_index('cp')
        positions = cp_idx * n_tok + jnp.arange(n_tok)
        queries, keys, values = attention_inputs(hidden, wq_attn, wk_attn, wv_attn, positions, head_dim)
        scale = 1.0 / math.sqrt(head_dim)
        tok_idx = jnp.arange(n_tok)
        causal = tok_idx[:, None] >= tok_idx[None, :]
        stats = softmax_update(softmax_init(queries), queries, keys, values, causal, scale)

        def kv_step(step_idx, state):
            run_stats, key_blk, value_blk = state
            key_blk, value_blk = lax.ppermute((key_blk, value_blk), 'cp', shift)
            run_stats = lax.cond(step_idx <= cp_idx, lambda prev: softmax_update(prev, queries, key_blk, value_blk, None, scale), lambda prev: prev, run_stats)
            return run_stats, key_blk, value_blk

        stats = lax.fori_loop(1, cp_size, kv_step, (stats, keys, values))[0]
        attn_sum = lax.psum(attention_partial(stats, wo_attn).astype(jnp.bfloat16), 'tp').astype(jnp.float32)
        mid_hidden = rms_norm(alphas[0] * hidden.astype(jnp.float32) + attn_sum, gain_attn).astype(jnp.bfloat16)

        lin_q, lin_k, lin_v, gate_vals = lightning_inputs(mid_hidden, wq_lin, wk_lin, wv_lin, wg_lin, n_heads)
        outputs, end_state = lightning_local(lin_q, lin_k, lin_v, slopes, tile)
        block_decay = jnp.exp(-slopes * n_tok)[None, :, None, None]

        def state_step(step_idx, state):
            incoming = lax.ppermute(state[1], 'cp', shift)
            return incoming, block_decay * incoming + end_state

        prior = lax.fori_loop(0, cp_size - 1, state_step, (jnp.zeros_like(end_state), end_state))[0]
        outputs = outputs + from_earlier(lin_q, prior, slopes)
        flat_out = outputs.reshape(gate_vals.shape)
        total_sq = lax.psum(jnp.sum(flat_out * flat_out, axis=-1, keepdims=True), 'tp')
        inner_vals = (flat_out * lax.rsqrt(total_sq / (flat_out.shape[-1] * tp_size) + NORM_EPS) * gain_inner * gate_vals).astype(jnp.bfloat16)
        lin_part = jnp.einsum('btn,nm->btm', inner_vals, wo_lin, preferred_element_type=jnp.float32)
        lin_sum = lax.psum(lin_part.astype(jnp.bfloat16), 'tp').astype(jnp.float32)
        return rms_norm(alphas[1] * mid_hidden.astype(jnp.float32) + lin_sum, gain_lin).astype(jnp.bfloat16)

    act_spec = P('dp', 'cp', None)
    rep_spec = P()
    col_spec = P(None, 'tp')
    row_spec = P('tp', None)
    vec_spec = P('tp')
    in_specs = (act_spec, rep_spec, col_spec, col_spec, col_spec, row_spec, rep_spec, col_spec, col_spec, col_spec, col_spec, vec_spec, vec_spec, row_spec, rep_spec)
    return jax.shard_map(body, mesh=mesh, in_specs=in_specs, out_specs=act_spec, check_vma=False)
```

profile of v0, /device:TPU:0, one launch (start us, length us, event | category | flops | bytes accessed | tf_op | source)
XLA Modules:
  0.0 4093.4 jit_solution(15047430011783823476)
XLA Ops:
  77.2 118.2 %fusion.23 = f32[16,128,4096]{2,1,0:T(8,128)} fusion(bf16[16,128,6144]{2,1,0:T(8,128)(2,1)} %param.21, bf16[6144,4096]{1,0:T(8,128)(2,1)} %param.23), kind=kOutput, calls=%fused_computation.27 | convolution fusion | flops 103079215104 | bytes 109051904 | tf_op jit(solution)/shard_map/btm,mn->btn/dot_general | solution.py:32
  386.8 260.2 %while.35 = (s32[]{:T(128)}, f32[16,4,8,128]{3,2,1,0:T(8,128)S(1)}, f32[16,4,8,128]{3,2,1,0:T(8,128)S(1)}, f32[16,4,8,128,128]{4,3,2,1,0:T(8,128)}, bf16[16,128,...) while((s32[]{:T(128)}, f32[16,4,8,128]{3,2,1,0:T(8,128)S(1)}, ...), condition=%wide.region_7.8_spmd.clone, body=%wide.region_2.7_spmd.sunk.clone | while | flops 4378984448 | bytes 218104096 | solution.py:131
  402.3 109.7 %collective-permute-start = (bf16[16,128,4,128]{3,1,2,0:T(8,128)(2,1)}, bf16[16,128,4,128]{3,1,2,0:T(8,128)(2,1)S(1)}, u32[]{:S(2)}, u32[]{:S(2)}) collective-permute-start(bf16[16,128,4,128]{3,1,2,0:T(8,128)(2,1)} %get-tuple-element.404), channel_id=1, source_target_pairs={{0,1},{1,2},{2,3},{4,5},{5,6},{6,7}} | collective-permute-start | bytes 6291464 | tf_op jit(solution)/shard_map/while/body/eval_jaxpr/ppermute | solution.py:127
  524.7 41.8 %collective-permute-start = (bf16[16,128,4,128]{3,1,2,0:T(8,128)(2,1)}, bf16[16,128,4,128]{3,1,2,0:T(8,128)(2,1)S(1)}, u32[]{:S(2)}, u32[]{:S(2)}) collective-permute-start(bf16[16,128,4,128]{3,1,2,0:T(8,128)(2,1)} %get-tuple-element.404), channel_id=1, source_target_pairs={{0,1},{1,2},{2,3},{4,5},{5,6},{6,7}} | collective-permute-start | bytes 6291464 | tf_op jit(solution)/shard_map/while/body/eval_jaxpr/ppermute | solution.py:127
  566.4 73.6 %collective-permute-start.1 = (bf16[16,128,4,128]{3,1,2,0:T(8,128)(2,1)}, bf16[16,128,4,128]{3,1,2,0:T(8,128)(2,1)}, u32[]{:S(2)}, u32[]{:S(2)}) collective-permute-start(bf16[16,128,4,128]{3,1,2,0:T(8,128)(2,1)} %get-tuple-element.405), channel_id=1, source_target_pairs={{0,1},{1,2},{2,3},{4,5},{5,6},{6,7}} | collective-permute-start | bytes 6291464 | tf_op jit(solution)/shard_map/while/body/eval_jaxpr/ppermute | solution.py:127
  647.0 120.2 %bitcast_convert_fusion = bf16[16,128,6144]{2,1,0:T(8,128)(2,1)} fusion(bf16[4,8,128,6144,1]{3,2,1,0,4:T(8,128)(2,1)} %bitcast.204, f32[16,4,8,128,128]{4,3,2,1,0:T(8,128)} %get-tuple-element.204, f32[16,4,8,128]{3,2,1,0:T(8,128)S(1)} %get-tuple-element.205), kind=kOutput, calls=%fused_computation.16 | convolution fusion | flops 103108575232 | bytes 109314048 | tf_op jit(solution)/shard_map/bkgqd,kgdm->bqm/dot_general | solution.py:61
  770.9 616.8 %all-reduce.3.cloned.1.call-done = bf16[16,128,6144]{2,1,0:T(8,128)(2,1)} async-done(((bf16[16,128,6144]{2,1,0:T(8,128)(2,1)}), bf16[16,128,6144]{2,1,0:T(8,128)(2,1)}) %all-reduce.3.cloned.1.call-update) | async-done | bytes 25165840 | tf_op jit(solution)/shard_map/psum | solution.py:132
  1440.7 122.7 %multiply_convert_fusion.3 = bf16[16,128,4096]{2,1,0:T(8,128)(2,1)} fusion(bf16[16,128,6144]{2,1,0:T(8,128)(2,1)} %multiply_convert_fusion.1, bf16[6144,4096]{1,0:T(8,128)(2,1)} %param.29), kind=kOutput, calls=%fused_computation.51 | convolution fusion | flops 103121158144 | bytes 92274688 | tf_op jit(solution)/shard_map/btm,mn->btn/dot_general | solution.py:69
  1584.5 123.1 %fusion.59 = bf16[16,16,32,8,128]{4,3,2,1,0:T(8,128)(2,1)} fusion(bf16[16,128,6144]{2,1,0:T(8,128)(2,1)} %multiply_convert_fusion.1, bf16[6144,4096]{1,0:T(8,128)(2,1)} %param.30), kind=kOutput, calls=%fused_computation.82 | convolution fusion | flops 103121158144 | bytes 92274688 | tf_op jit(solution)/shard_map/btm,mn->btn/dot_general | solution.py:69
  1707.7 123.7 %fusion.60 = bf16[16,16,32,8,128]{4,3,2,1,0:T(8,128)(2,1)} fusion(bf16[16,128,6144]{2,1,0:T(8,128)(2,1)} %multiply_convert_fusion.1, bf16[6144,4096]{1,0:T(8,128)(2,1)} %param.28), kind=kOutput, calls=%fused_computation.83 | convolution fusion | flops 103121158144 | bytes 92274688 | tf_op jit(solution)/shard_map/btm,mn->btn/dot_general | solution.py:69
  1831.4 31.7 broadcast_multiply_fusion
  1914.2 876.4 %while.36 = (s32[]{:T(128)}, f32[16,32,128,128]{3,2,1,0:T(8,128)}, f32[16,32,128,128]{3,2,1,0:T(8,128)}, f32[1,32,1,1]{1,3,2,0:T(1,128)S(1)}, f32[16,32,128,128]{3,2,1,0:T(8,128)}) while((s32[]{:T(128)}, f32[16,32,128,128]{3,2,1,0:T(8,128)}, f32[16,32,128,128]{3,2,1,0:T(8,128)}, f32[1,32,1,1]{1,3,2,0:T(1,128)S(1)}, ...), condition=%wide.region_11.12_spmd.clone, body=%wide.region_10.11_spmd.sunk.clone | while | flops 16777216 | bytes 234881264 | solution.py:143
  1926.5 37.9 collective-permute-done.2
  1964.4 32.6 multiply_add_fusion.5
  1997.1 326.0 %collective-permute-start.2 = (f32[16,32,128,128]{3,2,1,0:T(8,128)}, f32[16,32,128,128]{3,2,1,0:T(8,128)}, u32[]{:S(2)}, u32[]{:S(2)}) collective-permute-start(f32[16,32,128,128]{3,2,1,0:T(8,128)} %get-tuple-element.423), channel_id=1, source_target_pairs={{0,1},{1,2},{2,3},{4,5},{5,6},{6,7}} | collective-permute-start | bytes 100663304 | tf_op jit(solution)/shard_map/while/body/eval_jaxpr/ppermute | solution.py:140
  2323.0 37.9 collective-permute-done.2
  2361.0 32.6 multiply_add_fusion.5
  2393.6 326.5 %collective-permute-start.2 = (f32[16,32,128,128]{3,2,1,0:T(8,128)}, f32[16,32,128,128]{3,2,1,0:T(8,128)}, u32[]{:S(2)}, u32[]{:S(2)}) collective-permute-start(f32[16,32,128,128]{3,2,1,0:T(8,128)} %get-tuple-element.423), channel_id=1, source_target_pairs={{0,1},{1,2},{2,3},{4,5},{5,6},{6,7}} | collective-permute-start | bytes 100663304 | tf_op jit(solution)/shard_map/while/body/eval_jaxpr/ppermute | solution.py:140
  2720.1 37.9 collective-permute-done.2
  2758.0 32.6 multiply_add_fusion.5
  2818.9 49.7 %multiply_reduce_fusion.2 = (f32[16,128]{1,0:T(8,128)S(1)}, f32[16,128,32,128]{1,3,2,0:T(8,128)}) fusion(f32[128,32]{0,1:T(8,128)S(1)} %copy-done.6, f32[16,32,128,128]{3,2,1,0:T(8,128)} %fusion.42, f32[16,32,128,128]{3,2,1,0:T(8,128)} %fusion.28, bf16[16,128,32,128]{1,3,2,0:T(8,128)(2,1)} %bitcast.193, f32[32,128,128]{2,1,0:T(8,128)S(1)} %copy-done.2, ...), kind=kOutput, calls=%fused_computation.43 | convolution fusion | flops 4353685504 | bytes 153116672 | tf_op jit(solution)/shard_map/bnhqs,bnshd->bnqhd/dot_general | solution.py:87
  2905.4 118.1 %fusion.15 = f32[16,128,4096]{2,1,0:T(8,128)} fusion(bf16[16,128,6144]{2,1,0:T(8,128)(2,1)} %multiply_convert_fusion.1, bf16[6144,4096]{1,0:T(8,128)(2,1)} %param.31), kind=kOutput, calls=%fused_computation.19 | convolution fusion | flops 103079215104 | bytes 109051904 | tf_op jit(solution)/shard_map/btm,mn->btn/dot_general | solution.py:72
  3051.3 113.8 %fusion.68 = bf16[16,128,6144]{2,1,0:T(8,128)(2,1)} fusion(bf16[4096,6144]{1,0:T(8,128)(2,1)} %param.34, bf16[16,128,4096]{2,1,0:T(8,128)(2,1)} %multiply_convert_fusion.11), kind=kOutput, calls=%fused_computation.85 | convolution fusion | flops 103091798016 | bytes 92274688 | tf_op jit(solution)/shard_map/btn,nm->btm/dot_general | solution.py:148
  3165.1 868.2 %all-reduce.5.cloned.1.call-done = bf16[16,128,6144]{2,1,0:T(8,128)(2,1)} async-done(((bf16[16,128,6144]{2,1,0:T(8,128)(2,1)}), bf16[16,128,6144]{2,1,0:T(8,128)(2,1)}) %all-reduce.5.cloned.1.call-update) | async-done | bytes 25165840 | tf_op jit(solution)/shard_map/psum | solution.py:149
  (121 shorter events, 584.1 us)
Async XLA Ops:
  6.5 1381.2 %all-reduce.3.cloned.1.call-start = ((), (), s32[]{:S(2)}) async-start(), calls=%async_computation | async-start | bytes 50331648 | tf_op jit(solution)/shard_map/psum | solution.py:132
  232.9 28.4 copy-start.8
  324.3 31.2 copy-start
  386.8 8.6 collective-permute-start
  389.7 8.2 collective-permute-start.1
  402.3 115.3 %collective-permute-start = (bf16[16,128,4,128]{3,1,2,0:T(8,128)(2,1)}, bf16[16,128,4,128]{3,1,2,0:T(8,128)(2,1)S(1)}, u32[]{:S(2)}, u32[]{:S(2)}) collective-permute-start(bf16[16,128,4,128]{3,1,2,0:T(8,128)(2,1)} %get-tuple-element.404), channel_id=1, source_target_pairs={{0,1},{1,2},{2,3},{4,5},{5,6},{6,7}} | collective-permute-start | bytes 6291464 | tf_op jit(solution)/shard_map/while/body/eval_jaxpr/ppermute | solution.py:127
  512.1 8.1 collective-permute-start.1
  524.7 115.3 %collective-permute-start = (bf16[16,128,4,128]{3,1,2,0:T(8,128)(2,1)}, bf16[16,128,4,128]{3,1,2,0:T(8,128)(2,1)S(1)}, u32[]{:S(2)}, u32[]{:S(2)}) collective-permute-start(bf16[16,128,4,128]{3,1,2,0:T(8,128)(2,1)} %get-tuple-element.404), channel_id=1, source_target_pairs={{0,1},{1,2},{2,3},{4,5},{5,6},{6,7}} | collective-permute-start | bytes 6291464 | tf_op jit(solution)/shard_map/while/body/eval_jaxpr/ppermute | solution.py:127
  566.4 76.0 %collective-permute-start.1 = (bf16[16,128,4,128]{3,1,2,0:T(8,128)(2,1)}, bf16[16,128,4,128]{3,1,2,0:T(8,128)(2,1)}, u32[]{:S(2)}, u32[]{:S(2)}) collective-permute-start(bf16[16,128,4,128]{3,1,2,0:T(8,128)(2,1)} %get-tuple-element.405), channel_id=1, source_target_pairs={{0,1},{1,2},{2,3},{4,5},{5,6},{6,7}} | collective-permute-start | bytes 6291464 | tf_op jit(solution)/shard_map/while/body/eval_jaxpr/ppermute | solution.py:127
  647.0 120.3 %copy-start.17 = (f32[2]{0:T(128)S(1)}, f32[2]{0:T(128)}, u32[]{:S(2)}) copy-start(f32[2]{0:T(128)} %param.22) | copy-start | bytes 28
  647.0 120.9 %copy-start.20 = (f32[32]{0:T(128)S(1)}, f32[32]{0:T(128)}, u32[]{:S(2)}) copy-start(f32[32]{0:T(128)} %param.32) | copy-start | bytes 388
  767.2 642.0 %copy-start.12 = (f32[6144]{0:T(1024)S(1)}, f32[6144]{0:T(1024)}, u32[]{:S(2)}) copy-start(f32[6144]{0:T(1024)} %param.27) | copy-start | bytes 73732
  767.2 3266.2 %all-reduce.5.cloned.1.call-start = ((), (), s32[]{:S(2)}) async-start(), calls=%async_computation.1 | async-start | bytes 50331648 | tf_op jit(solution)/shard_map/psum | solution.py:149
  1707.7 123.7 %copy-start.10 = (f32[128,32]{0,1:T(8,128)S(1)}, f32[128,32]{0,1:T(8,128)}, u32[]{:S(2)}) copy-start(f32[128,32]{0,1:T(8,128)} %get-tuple-element.258) | copy-start | bytes 49156
  1707.7 123.7 %copy-start.16 = (f32[32]{0:T(128)S(1)}, f32[32]{0:T(128)}, u32[]{:S(2)}) copy-start(f32[32]{0:T(128)} %get-tuple-element.260) | copy-start | bytes 388
  1886.0 28.2 copy-start.14
  1914.2 50.2 %collective-permute-start.2 = (f32[16,32,128,128]{3,2,1,0:T(8,128)}, f32[16,32,128,128]{3,2,1,0:T(8,128)}, u32[]{:S(2)}, u32[]{:S(2)}) collective-permute-start(f32[16,32,128,128]{3,2,1,0:T(8,128)} %get-tuple-element.423), channel_id=1, source_target_pairs={{0,1},{1,2},{2,3},{4,5},{5,6},{6,7}} | collective-permute-start | bytes 100663304 | tf_op jit(solution)/shard_map/while/body/eval_jaxpr/ppermute | solution.py:140
  1997.1 363.9 %collective-permute-start.2 = (f32[16,32,128,128]{3,2,1,0:T(8,128)}, f32[16,32,128,128]{3,2,1,0:T(8,128)}, u32[]{:S(2)}, u32[]{:S(2)}) collective-permute-start(f32[16,32,128,128]{3,2,1,0:T(8,128)} %get-tuple-element.423), channel_id=1, source_target_pairs={{0,1},{1,2},{2,3},{4,5},{5,6},{6,7}} | collective-permute-start | bytes 100663304 | tf_op jit(solution)/shard_map/while/body/eval_jaxpr/ppermute | solution.py:140
  2393.6 364.4 %collective-permute-start.2 = (f32[16,32,128,128]{3,2,1,0:T(8,128)}, f32[16,32,128,128]{3,2,1,0:T(8,128)}, u32[]{:S(2)}, u32[]{:S(2)}) collective-permute-start(f32[16,32,128,128]{3,2,1,0:T(8,128)} %get-tuple-element.423), channel_id=1, source_target_pairs={{0,1},{1,2},{2,3},{4,5},{5,6},{6,7}} | collective-permute-start | bytes 100663304 | tf_op jit(solution)/shard_map/while/body/eval_jaxpr/ppermute | solution.py:140
  2790.6 28.3 copy-start.2
  2790.6 28.3 copy-start.6
  2905.4 118.1 %copy-start.11 = (f32[16,128]{1,0:T(8,128)S(1)}, f32[16,128]{1,0:T(8,128)}, u32[]{:S(2)}) copy-start(f32[16,128]{1,0:T(8,128)} %rsqrt_bitcast_fusion) | copy-start | bytes 24580
  2905.4 118.1 %copy-start.15 = (f32[4096]{0:T(1024)S(1)}, f32[4096]{0:T(1024)}, u32[]{:S(2)}) copy-start(f32[4096]{0:T(1024)} %param.33) | copy-start | bytes 49156
  3165.1 889.7 %copy-start.13 = (f32[6144]{0:T(1024)S(1)}, f32[6144]{0:T(1024)}, u32[]{:S(2)}) copy-start(f32[6144]{0:T(1024)} %param.35) | copy-start | bytes 73732
  (12 other events, 210.3 us)
Sparse Core Ops, SparseCore 0:
  767.3 620.3 all-reduce.2
  3165.3 868.0 all-reduce.4
where the time goes:
time: 4100 us; the launch traced here: 4090 us
  waiting for transfers between devices  1610 us (39%)
  matrix products  1070 us (26%)
  starting transfers between devices  904 us (22%)
  other arithmetic  307 us (7%)
  local copies, waits for them, and re-layouts  190 us (5%)
    psum x1, waiting for transfers between devices, body(): lin_sum = lax.psum(lin_part.astype(jnp.bfloat16), 'tp').astype(jnp.float32)  868 us
    ppermute x3, starting transfers between devices, state_step(): incoming = lax.ppermute(state[1], 'cp', shift)  665 us
    psum x1, waiting for transfers between devices, body(): lax.psum(attention_partial(stats, wo_attn).astype(jnp.bfloat16), 'tp')  617 us
    dot_general x3, matrix products, heads_of(): jnp.einsum('btm,mn->btn', mid_hidden, weight, preferred_element_type=jnp....  369 us
    ppermute x6, starting transfers between devices, kv_step(): key_blk, value_blk = lax.ppermute((key_blk, value_blk), 'cp', shift)  239 us
    dot_general x1, matrix products, attention_partial(): jnp.einsum('bkgqd,kgdm->bqm', attn_vals, w_out, preferred_element_type=jn...  120 us
    dot_general x1, matrix products, attention_inputs(): jnp.einsum('btm,mn->btn', hidden, wq_attn, preferred_element_type=jnp.flo...  118 us
    dot_general x1, matrix products, lightning_inputs(): jnp.einsum('btm,mn->btn', mid_hidden, wg_lin, preferred_element_type=jnp....  118 us
  transfers between devices with their start and end apart: 11, of which 8 were waited for; matrix products, arithmetic and copies ran while one was open for 0% of the time, Pallas kernels for 0%

commit v1 on v0

v1 whole, which is shorter than its diff:
```python
import math

import jax
import jax.numpy as jnp
import numpy as np
from jax import lax
from jax.experimental import pallas as pl
from jax.experimental.pallas import tpu as pltpu
from jax.sharding import PartitionSpec as P

MESH = pl.DeviceIdType.MESH
F32 = jnp.float32
BF = jnp.bfloat16
ROPE_BASE = 10000000.0
EPS = 1e-5

TOK = 128
HD = 128
TN = 512
DM = 6144
W = 4096
KVW = 1024
OWN_KV = W - KVW
N_SEQ = 4
N_CH = 4
N_CP = 4
N_G = 8
ROWS = N_SEQ * TOK
OWN = ROWS // 2
RB = 64
LA, LB = 0, 1
K, V, Q = 0, 1, 2
NT_DIMS = (((1,), (1,)), ((), ()))
TN_DIMS = (((0,), (0,)), ((), ()))


def rope_tables(n_cp):
    half = HD // 4
    inv = ROPE_BASE ** (-np.arange(half, dtype=np.float64) * 2.0 / (2 * half))
    pos = np.arange(n_cp * TOK, dtype=np.float64)
    ang = pos[:, None] * inv[None, :]
    tab = np.zeros((3, n_cp * TOK, HD), np.float32)
    tab[0] = 1.0
    tab[0, :, :half] = np.cos(ang)
    tab[0, :, half : 2 * half] = np.cos(ang)
    tab[1, :, :half] = -np.sin(ang)
    tab[2, :, half : 2 * half] = np.sin(ang)
    return np.ascontiguousarray(tab.reshape(3, n_cp, TOK, HD).transpose(1, 0, 2, 3))


def mo(v, m):
    return pl.multiple_of(v, m)


def parity(j):
    return lax.rem(j, 2)


def blk(b):
    return pl.ds(mo(b * TOK, TOK), TOK)


def hcol(g, hh):
    return pl.ds(mo((4 * g + hh) * HD, HD), HD)


def dot(a, b, dims=(((1,), (0,)), ((), ()))):
    return lax.dot_general(a, b, dims, preferred_element_type=F32)


def sigmoid(z):
    return 1.0 / (1.0 + jnp.exp(-z))


def kernel(
    hid, wqa, wka, wva, woa, wql, wkl, wvl, wgl, wol, rope_hbm, alphas, slopes, gains, ginner,
    out, pt, prec, h1own, h1oth, kvh, kvr, sth, str_,
    wbuf, x, kvq, gbuf, u, acc, ost, stg, pst, nb_p, nb_r, nb_h, nout, ss, rsb, rope, ssx, ssr, wtab,
    w_sem, x_sem, o_sem, kvo_sem, kvl_sem, sto_sem, stl_sem, nl_sem, no_sem,
    rs_send, rs_recv, ag_send, ag_recv, kv_send, kv_recv, st_send, st_recv, ss_send, ss_recv,
):
    cp = lax.axis_index("cp")
    tp = lax.axis_index("tp")
    mate = 1 - tp
    is0, is1, is2, is3 = (cp == c for c in range(N_CP))

    bar = pltpu.get_barrier_semaphore()
    pl.semaphore_signal(bar, inc=1, device_id={"tp": mate}, device_id_type=MESH)
    for d in range(1, 4):
        pl.semaphore_signal(bar, inc=1, device_id={"cp": lax.rem(cp + d, 4)}, device_id_type=MESH)

    def wcopy(src, col, slot, rows):
        dst = wbuf.at[slot] if rows == DM else wbuf.at[slot, pl.ds(0, rows)]
        return pltpu.make_async_copy(src.at[:, pl.ds(col, TN)], dst, w_sem.at[slot])

    def wcol(j):
        return mo(j * TN, TN)

    def issue_a(j, slot):
        @pl.when(j == 0)
        def _():
            wcopy(wka, 0, slot, DM).start()

        @pl.when(j == 1)
        def _():
            wcopy(wva, 0, slot, DM).start()

        @pl.when(j >= 2)
        def _():
            wcopy(wqa, wcol(j - 2), slot, DM).start()

    def issue_b(j, slot):
        for n, w in enumerate((wkl, wvl, wql, wgl)):

            @pl.when(j // 8 == n)
            def _(n=n, w=w):
                wcopy(w, wcol(j - 8 * n), slot, DM).start()

    def wait_w(slot, rows=DM):
        wcopy(wqa if rows == DM else woa, 0, slot, rows).wait()

    def own_row(i):
        return mo((tp * 8 + 2 * i) * TOK, TOK)

    def oth_row(i):
        return mo((mate * 8 + 2 * i) * TOK, TOK)

    def load_x(top, bot):
        a = pltpu.make_async_copy(top, x.at[pl.ds(0, OWN)], x_sem.at[0])
        b = pltpu.make_async_copy(bot, x.at[pl.ds(OWN, OWN)], x_sem.at[1])
        a.start()
        b.start()
        a.wait()
        b.wait()

    def rs_copy(n, i, col, width):
        return pltpu.make_async_remote_copy(
            src_ref=pt.at[n, i, pl.ds(OWN, OWN), pl.ds(col, width)],
            dst_ref=prec.at[n, i, :, pl.ds(col, width)],
            send_sem=rs_send.at[n, i],
            recv_sem=rs_recv.at[n, i],
            device_id={"tp": mate},
            device_id_type=MESH,
        )

    def ag_copy(n, i, row, rows):
        if n == 0:
            src = h1own.at[i, pl.ds(row, rows)]
            dst = h1oth.at[i, pl.ds(row, rows)]
        else:
            src = out.at[pl.ds(mo(own_row(i) + row, RB), rows)]
            dst = src
        return pltpu.make_async_remote_copy(
            src_ref=src,
            dst_ref=dst,
            send_sem=ag_send.at[n, i],
            recv_sem=ag_recv.at[n, i],
            device_id={"tp": mate},
            device_id_type=MESH,
        )

    def ag_wait_recv(n, i):
        if n == 0:
            ag_copy(0, i, 0, OWN).wait_recv()
        else:
            oth = out.at[pl.ds(oth_row(i), OWN)]
            pltpu.make_async_remote_copy(
                src_ref=oth,
                dst_ref=oth,
                send_sem=ag_send.at[n, i],
                recv_sem=ag_recv.at[n, i],
                device_id={"tp": mate},
                device_id_type=MESH,
            ).wait_recv()

    def kv_copy(i, src, own, dst_cp, send):
        return pltpu.make_async_remote_copy(
            src_ref=kvh.at[i] if own else kvr.at[i, src],
            dst_ref=kvr.at[i, src],
            send_sem=kv_send.at[i, send],
            recv_sem=kv_recv.at[i, src],
            device_id={"cp": dst_cp},
            device_id_type=MESH,
        )

    def st_copy(i, g):
        return pltpu.make_async_remote_copy(
            src_ref=sth.at[i, g],
            dst_ref=str_.at[i, g],
            send_sem=st_send.at[i, g],
            recv_sem=st_recv.at[i, g],
            device_id={"cp": lax.rem(cp + 1, 4)},
            device_id_type=MESH,
        )

    def ss_copy(i):
        return pltpu.make_async_remote_copy(
            src_ref=ssx.at[i],
            dst_ref=ssr.at[i],
            send_sem=ss_send.at[i],
            recv_sem=ss_recv.at[i],
            device_id={"tp": mate},
            device_id_type=MESH,
        )

    def norm(n, i):
        with jax.named_scope("norm_wait"):
            rs_copy(n, i, 0, DM).wait_recv()
        wait_n = n

        def loads(r, slot):
            rows = pl.ds(mo(r * RB, RB), RB)
            if wait_n == 0:
                res = hid.at[pl.ds(mo(own_row(i) + r * RB, RB), RB)]
            else:
                res = h1own.at[i, rows]
            return (
                pltpu.make_async_copy(pt.at[n, i, rows], nb_p.at[slot], nl_sem.at[slot, 0]),
                pltpu.make_async_copy(prec.at[n, i, rows], nb_r.at[slot], nl_sem.at[slot, 1]),
                pltpu.make_async_copy(res, nb_h.at[slot], nl_sem.at[slot, 2]),
            )

        def store(r, slot):
            rows = pl.ds(mo(r * RB, RB), RB)
            if n == 0:
                dst = h1own.at[i, rows]
            else:
                dst = out.at[pl.ds(mo(own_row(i) + r * RB, RB), RB)]
            return pltpu.make_async_copy(nout.at[slot], dst, no_sem.at[slot])

        with jax.named_scope("norm"):
            for c in loads(0, 0):
                c.start()
            alpha = alphas[n]

            @pl.loop(0, 4)
            def _(r):
                slot = parity(r)

                @pl.when(r + 1 < 4)
                def _():
                    for c in loads(r + 1, 1 - slot):
                        c.start()

                for c in loads(r, slot):
                    c.wait()

                @pl.loop(0, 4)
                def _(q):
                    rows = pl.ds(mo(q * 16, 16), 16)
                    both = nb_p[slot, rows, :].astype(F32) + nb_r[slot, rows, :].astype(F32)
                    h = alpha * nb_h[slot, rows, :].astype(F32) + both
                    inv = lax.rsqrt(jnp.mean(h * h, axis=-1, keepdims=True) + EPS)
                    nout[slot, rows, :] = (h * inv * gains[n : n + 1, :]).astype(BF)

                @pl.when(r >= 1)
                def _():
                    store(r - 1, 1 - slot).wait()
                    ag_copy(n, i, mo((r - 1) * RB, RB), RB).start()

                store(r, slot).start()

            store(3, 1).wait()
            ag_copy(n, i, OWN - RB, RB).start()

    def out_proj(n, i, wo, then):
        def put(j, slot):
            return pltpu.make_async_copy(ost.at[slot], pt.at[n, i, :, pl.ds(wcol(j), TN)], o_sem.at[slot])

        with jax.named_scope("out_proj"):
            @pl.loop(0, 12)
            def _(j):
                slot = parity(j)
                wait_w(slot, W)

                @pl.when(j + 1 < 12)
                def _():
                    wcopy(wo, wcol(j + 1), 1 - slot, W).start()

                @pl.when(j == 11)
                def _():
                    then()

                ost[slot] = dot(u[...], wbuf[slot, 0:W, :]).astype(BF)

                @pl.when(j >= 1)
                def _():
                    put(j - 1, 1 - slot).wait()
                    rs_copy(n, i, wcol(j - 1), TN).start()

                put(j, slot).start()

            put(11, 1).wait()
            rs_copy(n, i, 11 * TN, TN).start()

    def layer_a(i, then):
        with jax.named_scope("x_a"):
            load_x(hid.at[pl.ds(own_row(i), OWN)], hid.at[pl.ds(oth_row(i), OWN)])
        kv_out = pltpu.make_async_copy(kvq.at[K, :, pl.ds(OWN_KV, KVW)], kvh.at[i], kvo_sem)

        def finish(j, slot):
            kind = jnp.where(j == 1, 1, 0)
            dst = jnp.where(j < 2, 0, 2)
            col = mo(jnp.where(j < 2, OWN_KV + j * TN, (j - 2) * TN), TN)
            for b in range(N_SEQ):
                for h in range(N_SEQ):
                    a = acc[slot, blk(b), h * HD : (h + 1) * HD]
                    a = (
                        a * rope[kind, 0]
                        + pltpu.roll(a, HD - 32, 1) * rope[kind, 1]
                        + pltpu.roll(a, 32, 1) * rope[kind, 2]
                    )
                    kvq[dst, blk(b), pl.ds(col + h * HD, HD)] = a.astype(BF)

        with jax.named_scope("qkv_a"):
            @pl.loop(0, 10)
            def _(j):
                slot = parity(j)
                wait_w(slot)

                @pl.when(j + 1 < 10)
                def _():
                    issue_a(j + 1, 1 - slot)

                @pl.when(j == 9)
                def _():
                    wcopy(woa, 0, 0, W).start()

                finish(jnp.maximum(j - 1, 0), 1 - slot)
                acc[slot] = dot(x[...], wbuf[slot])

                @pl.when(j == 2)
                def _():
                    kv_out.start()

                @pl.when(j == 3)
                def _():
                    kv_out.wait()

                    @pl.when(is0)
                    def _():
                        kv_copy(i, 0, True, 2, 0).start()
                        kv_copy(i, 0, True, 1, 1).start()

                    @pl.when(is1)
                    def _():
                        kv_copy(i, 1, True, 3, 0).start()

                    @pl.when(is2)
                    def _():
                        kv_copy(i, 2, True, 3, 0).start()

        finish(9, 1)

        with jax.named_scope("kv_wait"):
            @pl.when(is2)
            def _():
                kv_copy(i, 0, False, 3, 1).wait_recv()
                kv_copy(i, 0, False, 3, 1).start()

            @pl.when(is3)
            def _():
                kv_copy(i, 1, False, 2, 0).wait_recv()
                kv_copy(i, 1, False, 2, 0).start()
                kv_copy(i, 2, False, 2, 0).wait_recv()
                kv_copy(i, 0, False, 2, 0).wait_recv()

            @pl.when(is2)
            def _():
                kv_copy(i, 1, False, 3, 1).wait_recv()

            @pl.when(is1)
            def _():
                kv_copy(i, 0, False, 3, 1).wait_recv()

            def kv_load(s):
                return pltpu.make_async_copy(kvr.at[i, s], kvq.at[K, :, pl.ds(s * KVW, KVW)], kvl_sem.at[s])

            for s in range(3):

                @pl.when(cp > s)
                def _(s=s):
                    kv_load(s).start()

            for s in range(3):

                @pl.when(cp > s)
                def _(s=s):
                    kv_load(s).wait()

        with jax.named_scope("attn"):
            scale = math.log2(math.e) / math.sqrt(HD)
            for c in range(N_SEQ):

                @pl.when(cp == c)
                def _(c=c):
                    cols = [OWN_KV] + [s * KVW for s in range(c)]

                    @pl.loop(0, 16)
                    def _(t):
                        b = t // 4
                        g = lax.rem(t, 4)
                        rows = blk(b)
                        ks = [kvq[K, rows, pl.ds(mo(o + g * HD, HD), HD)] for o in cols]
                        vs = [kvq[K, rows, pl.ds(mo(o + TN + g * HD, HD), HD)] for o in cols]
                        keys = jnp.concatenate(ks, axis=0) if c else ks[0]
                        vals = jnp.concatenate(vs, axis=0) if c else vs[0]
                        key_id = lax.broadcasted_iota(jnp.int32, (TOK, 2 * TOK), 0)
                        tok_id = lax.rem(lax.broadcasted_iota(jnp.int32, (TOK, 2 * TOK), 1), TOK)
                        causal = key_id <= tok_id
                        for p in range(N_SEQ):
                            hc = [mo((g * 8 + 2 * p + e) * HD, HD) for e in range(2)]
                            qs = jnp.concatenate([kvq[Q, rows, pl.ds(o, HD)] for o in hc], axis=0)
                            s = dot(keys, qs, NT_DIMS)
                            own = jnp.where(causal, s[:TOK], -jnp.inf)
                            s = jnp.concatenate([own, s[TOK:]], axis=0) if c else own
                            m = jnp.max(s, axis=0, keepdims=True)
                            e = jnp.exp2((s - m) * scale)
                            inv = 1.0 / jnp.sum(e, axis=0, keepdims=True)
                            o = dot(vals, e.astype(BF), TN_DIMS) * inv
                            for z in range(2):
                                u[rows, pl.ds(hc[z], HD)] = o[:, z * TOK : (z + 1) * TOK].T.astype(BF)

        out_proj(0, i, woa, then)

    def key_decay(h):
        back = lax.broadcasted_iota(jnp.int32, (TOK, HD), 0).astype(F32) - (TOK - 1.0)
        return jnp.exp(slopes[h] * back)

    def state_of(g, b, hh, kd):
        rows = blk(b)
        col = hcol(g, hh)
        k = (kvq[K, rows, col].astype(F32) * kd).astype(BF)
        return dot(k, kvq[V, rows, col], TN_DIMS)

    def block_decay(h):
        return jnp.exp(jnp.full((8, HD), -float(TOK), F32) * slopes[h])[0:1, :]

    def st_store(i, g, slot):
        return pltpu.make_async_copy(stg.at[slot], sth.at[i, g], sto_sem.at[slot])

    def st_load(i, g, slot):
        return pltpu.make_async_copy(str_.at[i, g], pst.at[slot], stl_sem.at[slot])

    def local_state(i, g):
        slot = parity(g)

        @pl.when(is1)
        def _():
            st_copy(i, g).wait_recv()
            st_load(i, g, slot).start()
            st_load(i, g, slot).wait()

        @pl.when(is0)
        def _():
            for hh in range(N_SEQ):
                kd = key_decay(4 * g + hh)
                for b in range(N_SEQ):
                    stg[slot, b * 4 + hh] = state_of(g, b, hh, kd)

        @pl.when(is1)
        def _():
            for hh in range(N_SEQ):
                kd = key_decay(4 * g + hh)
                bd = block_decay(4 * g + hh)
                for b in range(N_SEQ):
                    stg[slot, b * 4 + hh] = state_of(g, b, hh, kd) + bd * pst[slot, b * 4 + hh]

        st_store(i, g, slot).start()

    def st_send_on(i, g):
        st_store(i, g, parity(g)).wait()
        st_copy(i, g).start()

    def layer_b(i, middle, then):
        with jax.named_scope("h1_wait"):
            ag_wait_recv(0, i)
        with jax.named_scope("x_b"):
            load_x(h1own.at[i], h1oth.at[i])

        def finish(j, a):
            kvq[j // 8, :, pl.ds(wcol(lax.rem(j, 8)), TN)] = (a * sigmoid(a)).astype(BF)

        with jax.named_scope("qkv_b"):
            @pl.loop(0, 24)
            def _(j):
                slot = parity(j)
                wait_w(slot)
                issue_b(j + 1, 1 - slot)
                finish(j, dot(x[...], wbuf[slot]))

                @pl.when((cp <= 1) & (j >= 9) & (j < 17))
                def _():
                    local_state(i, j - 9)

                    @pl.when(j >= 10)
                    def _():
                        st_send_on(i, j - 10)

                @pl.when((cp <= 1) & (j == 17))
                def _():
                    st_send_on(i, 7)

        middle()

        with jax.named_scope("gate"):
            @pl.loop(0, 8)
            def _(j):
                slot = parity(j)
                wait_w(slot)

                @pl.when(j + 1 < 8)
                def _():
                    issue_b(25 + j, 1 - slot)

                @pl.when(j == 7)
                def _():
                    wcopy(wol, 0, 0, W).start()

                gbuf[:, pl.ds(wcol(j), TN)] = sigmoid(dot(x[...], wbuf[slot]))

        with jax.named_scope("lin"):
            ss[...] = jnp.zeros_like(ss)

            @pl.when(is0)
            def _():
                pst[...] = jnp.zeros_like(pst)

            @pl.loop(0, 8)
            def _(g):
                slot = parity(g)

                @pl.when(is1)
                def _():
                    st_load(i, g, slot).start()

                @pl.when(cp >= 2)
                def _():
                    st_copy(i, g).wait_recv()
                    st_load(i, g, slot).start()

                for hh in range(N_SEQ):
                    lam = slopes[4 * g + hh]
                    row = lax.broadcasted_iota(jnp.int32, (TOK, HD), 0).astype(F32)
                    lane = lax.broadcasted_iota(jnp.int32, (TOK, HD), 1).astype(F32)
                    gap = row - lane
                    wtab[hh, 0] = jnp.where(gap >= 0, jnp.exp(-lam * jnp.maximum(gap, 0.0)), 0.0)
                    wtab[hh, 1] = jnp.exp(-lam * (row + 1.0))

                @pl.when(cp >= 1)
                def _():
                    st_load(i, g, slot).wait()

                @pl.when(is2)
                def _():
                    for hh in range(N_SEQ):
                        kd = key_decay(4 * g + hh)
                        bd = block_decay(4 * g + hh)
                        for b in range(N_SEQ):
                            stg[slot, b * 4 + hh] = state_of(g, b, hh, kd) + bd * pst[slot, b * 4 + hh]
                    st_store(i, g, slot).start()

                @pl.loop(0, 4)
                def _(b):
                    rows = blk(b)
                    sq = None
                    res = []
                    for hh in range(N_SEQ):
                        col = hcol(g, hh)
                        q = kvq[Q, rows, col]
                        w = (dot(q, kvq[K, rows, col], NT_DIMS) * wtab[hh, 0]).astype(BF)
                        o = dot(w, kvq[V, rows, col])
                        o = o + dot(q, pst[slot, b * 4 + hh].astype(BF)) * wtab[hh, 1]
                        sq = o * o if sq is None else sq + o * o
                        res.append(o * ginner[0:1, col] * gbuf[rows, col])
                    for hh in range(N_SEQ):
                        gbuf[rows, hcol(g, hh)] = res[hh]
                    ss[rows, :] += sq

                @pl.when(is2)
                def _():
                    st_send_on(i, g)

        with jax.named_scope("ss_swap"):
            sums = [jnp.sum(ss[blk(b), :].T, axis=0, keepdims=True) for b in range(N_SEQ)]
            ssx[i] = jnp.concatenate(sums + sums, axis=0)
            ss_copy(i).start()
            ss_copy(i).wait_recv()
            for b in range(N_SEQ):
                whole = ssx[i, b : b + 1, :] + ssr[i, b ^ 2 : (b ^ 2) + 1, :]
                inv = lax.rsqrt(whole / 8192.0 + EPS)
                rsb[b] = jnp.broadcast_to(inv, (TOK, TOK)).T

        with jax.named_scope("scale"):
            @pl.loop(0, 8)
            def _(g):
                for b in range(N_SEQ):
                    rsv = rsb[b]
                    for hh in range(N_SEQ):
                        col = hcol(g, hh)
                        u[blk(b), col] = (gbuf[blk(b), col] * rsv).astype(BF)

        out_proj(1, i, wol, then)

    issue_a(0, 0)
    rope_in = pltpu.make_async_copy(rope_hbm.at[cp], rope.at[0], kvo_sem)
    rope_in.start()
    rope[1, 0] = jnp.ones((TOK, HD), F32)
    rope[1, 1] = jnp.zeros((TOK, HD), F32)
    rope[1, 2] = jnp.zeros((TOK, HD), F32)
    rope_in.wait()
    pl.semaphore_wait(bar, 4)

    @pl.loop(0, 7)
    def _(s):
        @pl.when((s < 3) | (s == 4))
        def _():
            def then_a():
                @pl.when(s < 2)
                def _():
                    issue_a(0, 0)

                @pl.when(s >= 2)
                def _():
                    issue_b(0, 0)

            layer_a(jnp.where(s < 3, s, 3), then_a)

        @pl.when((s == 1) | (s == 2))
        def _():
            norm(0, s - 1)

        @pl.when(s == 4)
        def _():
            norm(1, 0)

        @pl.when(s >= 3)
        def _():
            def middle():
                @pl.when(s <= 4)
                def _():
                    norm(0, s - 1)

                @pl.when(s >= 5)
                def _():
                    norm(1, s - 4)

            def then_b():
                @pl.when(s == 3)
                def _():
                    issue_a(0, 0)

                @pl.when((s > 3) & (s < 6))
                def _():
                    issue_b(0, 0)

            layer_b(s - 3, middle, then_b)

    norm(1, 3)

    for i in range(N_SEQ):
        for n in range(2):
            rs_copy(n, i, 0, DM).wait_send()
            ag_copy(n, i, 0, OWN).wait_send()
        ag_wait_recv(1, i)
        ss_copy(i).wait_send()

        @pl.when(is0)
        def _(i=i):
            kv_copy(i, 0, True, 2, 0).wait_send()
            kv_copy(i, 0, True, 1, 1).wait_send()

        @pl.when(is1)
        def _(i=i):
            kv_copy(i, 1, True, 3, 0).wait_send()

        @pl.when(is2)
        def _(i=i):
            kv_copy(i, 2, True, 3, 0).wait_send()
            kv_copy(i, 0, False, 3, 1).wait_send()

        @pl.when(is3)
        def _(i=i):
            kv_copy(i, 1, False, 2, 0).wait_send()

        @pl.when(cp <= 2)
        def _(i=i):
            @pl.loop(0, 8)
            def _(g):
                st_copy(i, g).wait_send()


def solution(mesh):
    n_cp = mesh.shape["cp"]
    table = rope_tables(n_cp)
    any_ = pl.BlockSpec(memory_space=pl.ANY)
    smem = pl.BlockSpec(memory_space=pltpu.SMEM)
    vmem = pl.BlockSpec(memory_space=pltpu.VMEM)
    dma = pltpu.SemaphoreType.DMA
    two = (2,)

    def body(hidden, alphas, wqa, wka, wva, woa, gain_attn, wql, wkl, wvl, wgl, slopes, gain_inner, wol, gain_lin):
        shape = hidden.shape
        hid = hidden.reshape(shape[0] * shape[1], shape[2])
        gains = jnp.stack([gain_attn, gain_lin])
        sds = jax.ShapeDtypeStruct
        outs = (
            sds(hid.shape, BF),
            sds((2, N_CH, ROWS, DM), BF),
            sds((2, N_CH, OWN, DM), BF),
            sds((N_CH, OWN, DM), BF),
            sds((N_CH, OWN, DM), BF),
            sds((N_CH, ROWS, KVW), BF),
            sds((N_CH, 3, ROWS, KVW), BF),
            sds((N_CH, N_G, 16, HD, HD), F32),
            sds((N_CH, N_G, 16, HD, HD), F32),
        )
        scratch = [
            pltpu.VMEM((2, DM, TN), BF),
            pltpu.VMEM((ROWS, DM), BF),
            pltpu.VMEM((3, ROWS, W), BF),
            pltpu.VMEM((ROWS, W), F32),
            pltpu.VMEM((ROWS, W), BF),
            pltpu.VMEM((2, ROWS, TN), F32),
            pltpu.VMEM((2, ROWS, TN), BF),
            pltpu.VMEM((2, 16, HD, HD), F32),
            pltpu.VMEM((2, 16, HD, HD), F32),
            pltpu.VMEM((2, RB, DM), BF),
            pltpu.VMEM((2, RB, DM), BF),
            pltpu.VMEM((2, RB, DM), BF),
            pltpu.VMEM((2, RB, DM), BF),
            pltpu.VMEM((ROWS, HD), F32),
            pltpu.VMEM((N_SEQ, TOK, HD), F32),
            pltpu.VMEM((2, 3, TOK, HD), F32),
            pltpu.VMEM((N_CH, 8, HD), F32),
            pltpu.VMEM((N_CH, 8, HD), F32),
            pltpu.VMEM((4, 2, TOK, HD), F32),
            dma(two), dma(two), dma(two), dma(()), dma((3,)), dma(two), dma(two), dma((2, 3)), dma(two),
            dma((2, N_CH)), dma((2, N_CH)), dma((2, N_CH)), dma((2, N_CH)), dma((N_CH, 2)), dma((N_CH, 3)), dma((N_CH, N_G)), dma((N_CH, N_G)),
            dma((N_CH,)), dma((N_CH,)),
        ]
        res = pl.pallas_call(
            kernel,
            out_shape=outs,
            in_specs=[any_] * 11 + [smem, smem, vmem, vmem],
            out_specs=tuple(any_ for _ in outs),
            scratch_shapes=scratch,
            compiler_params=pltpu.CompilerParams(
                collective_id=0, has_side_effects=True, vmem_limit_bytes=67043328
            ),
            name="layers",
        )(
            hid, wqa, wka, wva, woa, wql, wkl, wvl, wgl, wol, jnp.asarray(table), alphas, slopes, gains,
            gain_inner.reshape(1, -1),
        )
        return res[0].reshape(shape)

    act = P("dp", "cp", None)
    rep = P()
    col = P(None, "tp")
    row = P("tp", None)
    vec = P("tp")
    in_specs = (act, rep, col, col, col, row, rep, col, col, col, col, vec, vec, row, rep)
    return jax.shard_map(body, mesh=mesh, in_specs=in_specs, out_specs=act, check_vma=False)
```

time: 4100 us -> 1390 us (0.34)
  the two profiles are of different devices: /device:TPU:0 before, /device:TPU:6 now
where the time goes in v1:
time: 1390 us; the launch traced here: 1380 us
  Pallas kernels  1360 us (98%)
  local copies, waits for them, and re-layouts  21 us (2%)
    pallas_call x1, Pallas kernels, body(): pl.pallas_call(kernel, out_shape=outs, in_specs=[any_] * 11 + [smem, smem...  1360 us

profile of v1, /device:TPU:6, one launch (start us, length us, event | category | flops | bytes accessed | tf_op | source)
XLA Modules:
  0.0 1385.0 jit_solution(16876772990972863711)
XLA Ops:
  0.0 1.4 pad_maximum_fusion.gains
  1.4 1362.5 %layers.1 = (bf16[2048,6144]{1,0:T(8,128)(2,1)}, bf16[2,4,512,6144]{3,2,1,0:T(8,128)(2,1)}, bf16[2,4,256,6144]{3,2,1,0:T(8,128)(2,1)}, bf16[4,256,6144]{2,1,0:T(...) custom-call(bf16[2048,6144]{1,0:T(8,128)(2,1)} %bitcast.6, ...), custom_call_target="tpu_custom_call" | custom-call | tf_op jit(solution)/shard_map/layers/pallas_call | solution.py:742
  1364.0 21.0 %copy.18 = bf16[16,128,6144]{2,1,0:T(8,128)(2,1)} copy(bf16[16,128,6144]{2,1,0:T(8,128)(2,1)} %bitcast.5) | data formatting | bytes 50331648

commit v2 on v1

--- a/solution.py
+++ b/solution.py
@@ -27,7 +27,8 @@
 N_G = 8
 ROWS = N_SEQ * TOK
 OWN = ROWS // 2
-RB = 64
+RB = 32
+N_RB = OWN // RB
 LA, LB = 0, 1
 K, V, Q = 0, 1, 2
 NT_DIMS = (((1,), (1,)), ((), ()))
@@ -125,13 +126,26 @@
     def oth_row(i):
         return mo((mate * 8 + 2 * i) * TOK, TOK)
 
-    def load_x(top, bot):
-        a = pltpu.make_async_copy(top, x.at[pl.ds(0, OWN)], x_sem.at[0])
-        b = pltpu.make_async_copy(bot, x.at[pl.ds(OWN, OWN)], x_sem.at[1])
-        a.start()
-        b.start()
-        a.wait()
-        b.wait()
+    def x_copies(top, bot):
+        return (
+            pltpu.make_async_copy(top, x.at[pl.ds(0, OWN)], x_sem.at[0]),
+            pltpu.make_async_copy(bot, x.at[pl.ds(OWN, OWN)], x_sem.at[1]),
+        )
+
+    def x_from_hid(i):
+        return x_copies(hid.at[pl.ds(own_row(i), OWN)], hid.at[pl.ds(oth_row(i), OWN)])
+
+    def x_from_h1(i):
+        return x_copies(h1own.at[i], h1oth.at[i])
+
+    def start_x_a(i):
+        for c in x_from_hid(i):
+            c.start()
+
+    def start_x_b(i):
+        ag_wait_recv(LA, i)
+        for c in x_from_h1(i):
+            c.start()
 
     def rs_copy(n, i, col, width):
         return pltpu.make_async_remote_copy(
@@ -203,67 +217,99 @@
             device_id_type=MESH,
         )
 
-    def norm(n, i):
+    def norm_loads(n, i, r, start):
+        slot = parity(r)
+        rows = pl.ds(mo(r * RB, RB), RB)
+        copies = [
+            pltpu.make_async_copy(pt.at[n, i, rows], nb_p.at[slot], nl_sem.at[slot, 0]),
+            pltpu.make_async_copy(prec.at[n, i, rows], nb_r.at[slot], nl_sem.at[slot, 1]),
+        ]
+        res_a = hid.at[pl.ds(mo(own_row(i) + r * RB, RB), RB)]
+        res_b = h1own.at[i, rows]
+        for layer, res in ((LA, res_a), (LB, res_b)):
+
+            @pl.when(n == layer)
+            def _(res=res):
+                c = pltpu.make_async_copy(res, nb_h.at[slot], nl_sem.at[slot, 2])
+                c.start() if start else c.wait()
+
+        for c in copies:
+            c.start() if start else c.wait()
+
+    def norm_begin(n, i):
         with jax.named_scope("norm_wait"):
             rs_copy(n, i, 0, DM).wait_recv()
-        wait_n = n
-
-        def loads(r, slot):
-            rows = pl.ds(mo(r * RB, RB), RB)
-            if wait_n == 0:
-                res = hid.at[pl.ds(mo(own_row(i) + r * RB, RB), RB)]
-            else:
-                res = h1own.at[i, rows]
-            return (
-                pltpu.make_async_copy(pt.at[n, i, rows], nb_p.at[slot], nl_sem.at[slot, 0]),
-                pltpu.make_async_copy(prec.at[n, i, rows], nb_r.at[slot], nl_sem.at[slot, 1]),
-                pltpu.make_async_copy(res, nb_h.at[slot], nl_sem.at[slot, 2]),
-            )
-
-        def store(r, slot):
-            rows = pl.ds(mo(r * RB, RB), RB)
-            if n == 0:
-                dst = h1own.at[i, rows]
-            else:
-                dst = out.at[pl.ds(mo(own_row(i) + r * RB, RB), RB)]
-            return pltpu.make_async_copy(nout.at[slot], dst, no_sem.at[slot])
-
+
+            @pl.when(n == LB)
+            def _():
+                ss_copy(i).wait_recv()
+                for b in range(2):
+                    whole = ssx[i, b : b + 1, :] + ssr[i, b + 2 : b + 3, :]
+                    inv = lax.rsqrt(whole / float(2 * W) + EPS)
+                    rsb[blk(b), :] = jnp.broadcast_to(inv, (TOK, TOK)).T
+
+            @pl.when(n == LA)
+            def _():
+                rsb[...] = jnp.ones_like(rsb)
+
+            norm_loads(n, i, 0, True)
+
+    def norm_ready(n, i, r):
+        @pl.when(r + 1 < N_RB)
+        def _():
+            norm_loads(n, i, r + 1, True)
+
+        norm_loads(n, i, r, False)
+
+    def norm_rows(n, r):
+        slot = parity(r)
+        alpha = alphas[n]
+        for q in range(RB // 16):
+            rows = slice(q * 16, (q + 1) * 16)
+            both = nb_p[slot, rows, :].astype(F32) + nb_r[slot, rows, :].astype(F32)
+            both = both * rsb[pl.ds(mo(r * RB + q * 16, 16), 16), 0:1]
+            h = alpha * nb_h[slot, rows, :].astype(F32) + both
+            inv = lax.rsqrt(jnp.mean(h * h, axis=-1, keepdims=True) + EPS)
+            nout[slot, rows, :] = (h * inv * gains[pl.ds(n, 1), :]).astype(BF)
+
+    def norm_store(n, i, r, start):
+        slot = parity(r)
+        dst_a = h1own.at[i, pl.ds(mo(r * RB, RB), RB)]
+        dst_b = out.at[pl.ds(mo(own_row(i) + r * RB, RB), RB)]
+        for layer, dst in ((LA, dst_a), (LB, dst_b)):
+
+            @pl.when(n == layer)
+            def _(layer=layer, dst=dst):
+                c = pltpu.make_async_copy(nout.at[slot], dst, no_sem.at[slot])
+                if start:
+                    c.start()
+                else:
+                    c.wait()
+                    ag_copy(layer, i, mo(r * RB, RB), RB).start()
+
+    def norm_out(n, i, r):
+        @pl.when(r >= 1)
+        def _():
+            norm_store(n, i, r - 1, False)
+
+        norm_store(n, i, r, True)
+
+    def norm_end(n, i):
+        norm_store(n, i, N_RB - 1, False)
+
+    def norm(n, i):
+        norm_begin(n, i)
         with jax.named_scope("norm"):
-            for c in loads(0, 0):
-                c.start()
-            alpha = alphas[n]
-
-            @pl.loop(0, 4)
+
+            @pl.loop(0, N_RB)
             def _(r):
-                slot = parity(r)
-
-                @pl.when(r + 1 < 4)
-                def _():
-                    for c in loads(r + 1, 1 - slot):
-                        c.start()
-
-                for c in loads(r, slot):
-                    c.wait()
-
-                @pl.loop(0, 4)
-                def _(q):
-                    rows = pl.ds(mo(q * 16, 16), 16)
-                    both = nb_p[slot, rows, :].astype(F32) + nb_r[slot, rows, :].astype(F32)
-                    h = alpha * nb_h[slot, rows, :].astype(F32) + both
-                    inv = lax.rsqrt(jnp.mean(h * h, axis=-1, keepdims=True) + EPS)
-                    nout[slot, rows, :] = (h * inv * gains[n : n + 1, :]).astype(BF)
-
-                @pl.when(r >= 1)
-                def _():
-                    store(r - 1, 1 - slot).wait()
-                    ag_copy(n, i, mo((r - 1) * RB, RB), RB).start()
-
-                store(r, slot).start()
-
-            store(3, 1).wait()
-            ag_copy(n, i, OWN - RB, RB).start()
-
-    def out_proj(n, i, wo, then):
+                norm_ready(n, i, r)
+                norm_rows(n, r)
+                norm_out(n, i, r)
+
+            norm_end(n, i)
+
+    def out_proj(n, i, wo, then, pre):
         def put(j, slot):
             return pltpu.make_async_copy(ost.at[slot], pt.at[n, i, :, pl.ds(wcol(j), TN)], o_sem.at[slot])
 
@@ -281,6 +327,10 @@
                 def _():
                     then()
 
+                @pl.when(j == 8)
+                def _():
+                    pre()
+
                 ost[slot] = dot(u[...], wbuf[slot, 0:W, :]).astype(BF)
 
                 @pl.when(j >= 1)
@@ -293,9 +343,10 @@
             put(11, 1).wait()
             rs_copy(n, i, 11 * TN, TN).start()
 
-    def layer_a(i, then):
+    def layer_a(i, mid, then, pre):
         with jax.named_scope("x_a"):
-            load_x(hid.at[pl.ds(own_row(i), OWN)], hid.at[pl.ds(oth_row(i), OWN)])
+            for c in x_from_hid(i):
+                c.wait()
         kv_out = pltpu.make_async_copy(kvq.at[K, :, pl.ds(OWN_KV, KVW)], kvh.at[i], kvo_sem)
 
         def finish(j, slot):
@@ -328,6 +379,7 @@
 
                 finish(jnp.maximum(j - 1, 0), 1 - slot)
                 acc[slot] = dot(x[...], wbuf[slot])
+                mid(j)
 
                 @pl.when(j == 2)
                 def _():
@@ -405,23 +457,27 @@
                         vs = [kvq[K, rows, pl.ds(mo(o + TN + g * HD, HD), HD)] for o in cols]
                         keys = jnp.concatenate(ks, axis=0) if c else ks[0]
                         vals = jnp.concatenate(vs, axis=0) if c else vs[0]
-                        key_id = lax.broadcasted_iota(jnp.int32, (TOK, 2 * TOK), 0)
-                        tok_id = lax.rem(lax.broadcasted_iota(jnp.int32, (TOK, 2 * TOK), 1), TOK)
-                        causal = key_id <= tok_id
+                        row = lax.rem(lax.broadcasted_iota(jnp.int32, (2 * TOK, TOK), 0), TOK)
+                        causal = lax.broadcasted_iota(jnp.int32, (2 * TOK, TOK), 1) <= row
+
+                        def heads(p):
+                            return [pl.ds(mo((g * 8 + 2 * p + z) * HD, HD), HD) for z in range(2)]
+
+                        scores = []
                         for p in range(N_SEQ):
-                            hc = [mo((g * 8 + 2 * p + e) * HD, HD) for e in range(2)]
-                            qs = jnp.concatenate([kvq[Q, rows, pl.ds(o, HD)] for o in hc], axis=0)
-                            s = dot(keys, qs, NT_DIMS)
-                            own = jnp.where(causal, s[:TOK], -jnp.inf)
-                            s = jnp.concatenate([own, s[TOK:]], axis=0) if c else own
-                            m = jnp.max(s, axis=0, keepdims=True)
+                            qs = jnp.concatenate([kvq[Q, rows, o] for o in heads(p)], axis=0)
+                            scores.append(dot(qs, keys, NT_DIMS))
+                        for p in range(N_SEQ):
+                            s = scores[p]
+                            own = jnp.where(causal, s[:, :TOK], -jnp.inf)
+                            s = jnp.concatenate([own, s[:, TOK:]], axis=1) if c else own
+                            m = jnp.max(s, axis=1, keepdims=True)
                             e = jnp.exp2((s - m) * scale)
-                            inv = 1.0 / jnp.sum(e, axis=0, keepdims=True)
-                            o = dot(vals, e.astype(BF), TN_DIMS) * inv
+                            o = dot(e.astype(BF), vals) * (1.0 / jnp.sum(e, axis=1, keepdims=True))
                             for z in range(2):
-                                u[rows, pl.ds(hc[z], HD)] = o[:, z * TOK : (z + 1) * TOK].T.astype(BF)
-
-        out_proj(0, i, woa, then)
+                                u[rows, heads(p)[z]] = o[z * TOK : (z + 1) * TOK].astype(BF)
+
+        out_proj(0, i, woa, then, pre)
 
     def key_decay(h):
         back = lax.broadcasted_iota(jnp.int32, (TOK, HD), 0).astype(F32) - (TOK - 1.0)
@@ -442,6 +498,14 @@
     def st_load(i, g, slot):
         return pltpu.make_async_copy(str_.at[i, g], pst.at[slot], stl_sem.at[slot])
 
+    def next_state(g):
+        slot = parity(g)
+        for hh in range(4):
+            kd = key_decay(4 * g + hh)
+            bd = block_decay(4 * g + hh)
+            for b in range(N_SEQ):
+                stg[slot, b * 4 + hh] = state_of(g, b, hh, kd) + bd * pst[slot, b * 4 + hh]
+
     def local_state(i, g):
         slot = parity(g)
 
@@ -472,11 +536,10 @@
         st_store(i, g, parity(g)).wait()
         st_copy(i, g).start()
 
-    def layer_b(i, middle, then):
-        with jax.named_scope("h1_wait"):
-            ag_wait_recv(0, i)
+    def layer_b(i, mid, then, pre):
         with jax.named_scope("x_b"):
-            load_x(h1own.at[i], h1oth.at[i])
+            for c in x_from_h1(i):
+                c.wait()
 
         def finish(j, a):
             kvq[j // 8, :, pl.ds(wcol(lax.rem(j, 8)), TN)] = (a * sigmoid(a)).astype(BF)
@@ -501,9 +564,10 @@
                 def _():
                     st_send_on(i, 7)
 
-        middle()
+                mid(j)
 
         with jax.named_scope("gate"):
+
             @pl.loop(0, 8)
             def _(j):
                 slot = parity(j)
@@ -517,29 +581,55 @@
                 def _():
                     wcopy(wol, 0, 0, W).start()
 
+                @pl.when(is2)
+                def _():
+                    st_copy(i, j).wait_recv()
+                    st_load(i, j, slot).start()
+
                 gbuf[:, pl.ds(wcol(j), TN)] = sigmoid(dot(x[...], wbuf[slot]))
 
+                @pl.when(is2)
+                def _():
+                    st_load(i, j, slot).wait()
+                    next_state(j)
+                    st_store(i, j, slot).start()
+
+                    @pl.when(j >= 1)
+                    def _():
+                        st_send_on(i, j - 1)
+
         with jax.named_scope("lin"):
+
+            @pl.when(is2)
+            def _():
+                st_send_on(i, N_G - 1)
+
             ss[...] = jnp.zeros_like(ss)
+
+            def fetch(g):
+                @pl.when(is3)
+                def _():
+                    st_copy(i, g).wait_recv()
+
+                @pl.when(cp >= 1)
+                def _():
+                    st_load(i, g, parity(g)).start()
 
             @pl.when(is0)
             def _():
                 pst[...] = jnp.zeros_like(pst)
 
-            @pl.loop(0, 8)
+            fetch(0)
+
+            @pl.loop(0, N_G)
             def _(g):
                 slot = parity(g)
 
-                @pl.when(is1)
-                def _():
-                    st_load(i, g, slot).start()
-
-                @pl.when(cp >= 2)
-                def _():
-                    st_copy(i, g).wait_recv()
-                    st_load(i, g, slot).start()
-
-                for hh in range(N_SEQ):
+                @pl.when(g + 1 < N_G)
+                def _():
+                    fetch(g + 1)
+
+                for hh in range(4):
                     lam = slopes[4 * g + hh]
                     row = lax.broadcasted_iota(jnp.int32, (TOK, HD), 0).astype(F32)
                     lane = lax.broadcasted_iota(jnp.int32, (TOK, HD), 1).astype(F32)
@@ -551,58 +641,33 @@
                 def _():
                     st_load(i, g, slot).wait()
 
-                @pl.when(is2)
-                def _():
-                    for hh in range(N_SEQ):
-                        kd = key_decay(4 * g + hh)
-                        bd = block_decay(4 * g + hh)
-                        for b in range(N_SEQ):
-                            stg[slot, b * 4 + hh] = state_of(g, b, hh, kd) + bd * pst[slot, b * 4 + hh]
-                    st_store(i, g, slot).start()
-
-                @pl.loop(0, 4)
-                def _(b):
-                    rows = blk(b)
-                    sq = None
-                    res = []
-                    for hh in range(N_SEQ):
-                        col = hcol(g, hh)
-                        q = kvq[Q, rows, col]
-                        w = (dot(q, kvq[K, rows, col], NT_DIMS) * wtab[hh, 0]).astype(BF)
-                        o = dot(w, kvq[V, rows, col])
-                        o = o + dot(q, pst[slot, b * 4 + hh].astype(BF)) * wtab[hh, 1]
-                        sq = o * o if sq is None else sq + o * o
-                        res.append(o * ginner[0:1, col] * gbuf[rows, col])
-                    for hh in range(N_SEQ):
-                        gbuf[rows, hcol(g, hh)] = res[hh]
-                    ss[rows, :] += sq
-
-                @pl.when(is2)
-                def _():
-                    st_send_on(i, g)
-
-        with jax.named_scope("ss_swap"):
+                @pl.loop(0, 2)
+                def _(half):
+                    pairs = [(half * 2 + z, hh) for z in range(2) for hh in range(4)]
+                    at = [(blk(b), hcol(g, hh)) for b, hh in pairs]
+                    qs = [kvq[Q, r, c] for r, c in at]
+                    inner = [dot(q, kvq[K, r, c], NT_DIMS) for q, (r, c) in zip(qs, at)]
+                    prior = [dot(q, pst[slot, b * 4 + hh].astype(BF)) for q, (b, hh) in zip(qs, pairs)]
+                    o = [
+                        dot((s * wtab[hh, 0]).astype(BF), kvq[V, r, c]) + p * wtab[hh, 1]
+                        for s, p, (r, c), (b, hh) in zip(inner, prior, at, pairs)
+                    ]
+                    for v, (r, c) in zip(o, at):
+                        u[r, c] = (v * ginner[0:1, c] * gbuf[r, c]).astype(BF)
+                    for z in range(2):
+                        ss[at[4 * z][0], :] += sum(v * v for v in o[4 * z : 4 * z + 4])
+
             sums = [jnp.sum(ss[blk(b), :].T, axis=0, keepdims=True) for b in range(N_SEQ)]
             ssx[i] = jnp.concatenate(sums + sums, axis=0)
+
+        def then_ss():
             ss_copy(i).start()
-            ss_copy(i).wait_recv()
-            for b in range(N_SEQ):
-                whole = ssx[i, b : b + 1, :] + ssr[i, b ^ 2 : (b ^ 2) + 1, :]
-                inv = lax.rsqrt(whole / 8192.0 + EPS)
-                rsb[b] = jnp.broadcast_to(inv, (TOK, TOK)).T
-
-        with jax.named_scope("scale"):
-            @pl.loop(0, 8)
-            def _(g):
-                for b in range(N_SEQ):
-                    rsv = rsb[b]
-                    for hh in range(N_SEQ):
-                        col = hcol(g, hh)
-                        u[blk(b), col] = (gbuf[blk(b), col] * rsv).astype(BF)
-
-        out_proj(1, i, wol, then)
+            pre()
+
+        out_proj(1, i, wol, then, then_ss)
 
     issue_a(0, 0)
+    start_x_a(0)
     rope_in = pltpu.make_async_copy(rope_hbm.at[cp], rope.at[0], kvo_sem)
     rope_in.start()
     rope[1, 0] = jnp.ones((TOK, HD), F32)
@@ -615,6 +680,11 @@
     def _(s):
         @pl.when((s < 3) | (s == 4))
         def _():
+            def mid_a(j):
+                @pl.when((s == 1) & (j == 6))
+                def _():
+                    norm(LA, 0)
+
             def then_a():
                 @pl.when(s < 2)
                 def _():
@@ -624,26 +694,29 @@
                 def _():
                     issue_b(0, 0)
 
-            layer_a(jnp.where(s < 3, s, 3), then_a)
-
-        @pl.when((s == 1) | (s == 2))
-        def _():
-            norm(0, s - 1)
-
-        @pl.when(s == 4)
-        def _():
-            norm(1, 0)
+            def pre_a():
+                @pl.when(s < 2)
+                def _():
+                    start_x_a(s + 1)
+
+                @pl.when(s >= 2)
+                def _():
+                    start_x_b(jnp.where(s == 2, 0, 1))
+
+            layer_a(jnp.where(s < 3, s, 3), mid_a, then_a, pre_a)
+
+        @pl.when(s == 2)
+        def _():
+            norm(LA, 1)
 
         @pl.when(s >= 3)
         def _():
-            def middle():
-                @pl.when(s <= 4)
-                def _():
-                    norm(0, s - 1)
-
-                @pl.when(s >= 5)
-                def _():
-                    norm(1, s - 4)
+            def mid_b(j):
+                now = jnp.where(s == 4, 0, jnp.where(s == 6, 19, 15))
+
+                @pl.when(j == now)
+                def _():
+                    norm(jnp.where(s == 3, LA, LB), jnp.where(s == 3, 2, s - 4))
 
             def then_b():
                 @pl.when(s == 3)
@@ -654,9 +727,22 @@
                 def _():
                     issue_b(0, 0)
 
-            layer_b(s - 3, middle, then_b)
-
-    norm(1, 3)
+            def pre_b():
+                @pl.when(s == 3)
+                def _():
+                    start_x_a(3)
+
+                @pl.when((s > 3) & (s < 6))
+                def _():
+                    start_x_b(s - 2)
+
+            layer_b(s - 3, mid_b, then_b, pre_b)
+
+        @pl.when(s == 4)
+        def _():
+            norm(LA, 3)
+
+    norm(LB, 3)
 
     for i in range(N_SEQ):
         for n in range(2):
@@ -730,7 +816,7 @@
             pltpu.VMEM((2, RB, DM), BF),
             pltpu.VMEM((2, RB, DM), BF),
             pltpu.VMEM((ROWS, HD), F32),
-            pltpu.VMEM((N_SEQ, TOK, HD), F32),
+            pltpu.VMEM((OWN, HD), F32),
             pltpu.VMEM((2, 3, TOK, HD), F32),
             pltpu.VMEM((N_CH, 8, HD), F32),
             pltpu.VMEM((N_CH, 8, HD), F32),

time: 1390 us -> 1220 us (0.88)
  the two profiles are of different devices: /device:TPU:6 before, /device:TPU:2 now
where the time goes in v2:
time: 1220 us; the launch traced here: 1210 us
  Pallas kernels  1190 us (98%)
  local copies, waits for them, and re-layouts  21 us (2%)
    pallas_call x1, Pallas kernels, body(): pl.pallas_call(kernel, out_shape=outs, in_specs=[any_] * 11 + [smem, smem...  1190 us

profile of v2, /device:TPU:2, one launch (start us, length us, event | category | flops | bytes accessed | tf_op | source)
XLA Modules:
  0.0 1212.7 jit_solution(9850036464442092762)
XLA Ops:
  0.0 1.4 pad_maximum_fusion.gains
  1.4 1190.2 %layers.1 = (bf16[2048,6144]{1,0:T(8,128)(2,1)}, bf16[2,4,512,6144]{3,2,1,0:T(8,128)(2,1)}, bf16[2,4,256,6144]{3,2,1,0:T(8,128)(2,1)}, bf16[4,256,6144]{2,1,0:T(...) custom-call(bf16[2048,6144]{1,0:T(8,128)(2,1)} %bitcast.6, ...), custom_call_target="tpu_custom_call" | custom-call | tf_op jit(solution)/shard_map/layers/pallas_call | solution.py:828
  1191.7 21.0 %copy.18 = bf16[16,128,6144]{2,1,0:T(8,128)(2,1)} copy(bf16[16,128,6144]{2,1,0:T(8,128)(2,1)} %bitcast.5) | data formatting | bytes 50331648
